TPU v7x, 32 devices: a whole 2x2x4 slice. The times are simulated.
32 devices in a mesh: tm: 8 (over z, y), chan: 4 (over x, core).
Axes of the slice: x: 2, y: 2, z: 4, core: 2. Of those that a mesh axis runs over, the one named last changes fastest.
Arguments:
- coarse: bfloat16 [2, 24576, 4096], P(None, 'tm', 'chan'), may hold values from -6 to 6
- prototype: float32 [16, 1024], replicated, may hold values from -4 to 4
- req_block: int32 [4, 4], replicated, may hold values from 0 to 31, as said below
- req_start: int32 [4, 4], replicated, may hold values from 0 to 8, as said below
- req_frames: int32 [4, 4], replicated, may hold values from 1 to 9
- req_count: int32 [4], replicated, may hold values from 1 to 4, as said below
Outputs:
- spectra: bfloat16 [24, 4, 4, 2, 1024, 128], P('tm', 'chan')
Inputs may be any that keep to these rules, and one draw needn't show every extreme that they name: `req_block`: among the live slots of one owner at most 2 name blocks b with the same b // 8; in every draw some owner reaches 2. req_start + req_frames <= 9 in every slot; in every draw some live slot starts at hop 9 - 1 and some live slot spans all 9 frames. Slots q < req_count[c] of owner c are live, the others are empty; in every draw some owner has 4 live slots.
All inputs are finite; a program needn't handle non-finite values.
Results may differ from a plain program's by a relative error of at most 0.001.
Values may be sent and summed in bfloat16 or wider, within the bound.
A program may use at most 256 MiB of HBM per device.

v0:
```python
import functools
import math

import jax
import jax.numpy as jnp
from jax import lax
from jax.experimental import pallas as pl
from jax.experimental.pallas import tpu as pltpu
from jax.sharding import PartitionSpec as P

BLOCKW = 128
NFINE = 1024
TAPS = 16
MAXREQ = 4
PAIR = 2
ROWS = 128
STEP = 16
ANY = pl.BlockSpec(memory_space=pl.ANY)


def build_table():
    line = jnp.arange(NFINE, dtype=jnp.int32)
    products = line[:, None] * line[None, :] % NFINE
    angles = products.astype(jnp.float32) * (2.0 * math.pi / NFINE)
    scale = 1.0 / math.sqrt(NFINE)
    return jnp.concatenate([jnp.cos(angles) * scale, jnp.sin(angles) * scale], axis=0)


def pack_kernel(chosen, coarse_ref, out_ref):
    out_ref[...] = coarse_ref[...].reshape(out_ref.shape)


def pack(coarse, chosen, first, hops):
    count = chosen.shape[0]
    return pl.pallas_call(
        pack_kernel,
        out_shape=jax.ShapeDtypeStruct((count, 2, hops * NFINE, BLOCKW), coarse.dtype),
        grid_spec=pltpu.PrefetchScalarGridSpec(
            num_scalar_prefetch=1,
            grid=(count,),
            in_specs=[pl.BlockSpec((2, hops * NFINE, BLOCKW), lambda i, c: (0, first, c[i]))],
            out_specs=pl.BlockSpec((1, 2, hops * NFINE, BLOCKW), lambda i, c: (i, 0, 0, 0)),
        ),
        cost_estimate=pl.CostEstimate(
            flops=0, transcendentals=0, bytes_accessed=count * 8 * hops * NFINE * BLOCKW
        ),
    )(chosen, coarse)


def select_kernel(pieces, arrival, in_ref, out_ref):
    share = BLOCKW // pieces
    for piece in range(pieces):
        cols = slice(piece * share, (piece + 1) * share)
        out_ref[piece] = jnp.concatenate([in_ref[0, 0, :, cols], in_ref[0, 1, :, cols]], axis=-1)


def select(incoming, arrival, pieces, hops):
    width = 2 * BLOCKW // pieces
    rows = hops * NFINE
    return pl.pallas_call(
        functools.partial(select_kernel, pieces),
        out_shape=jax.ShapeDtypeStruct((MAXREQ * pieces, rows, width), incoming.dtype),
        grid_spec=pltpu.PrefetchScalarGridSpec(
            num_scalar_prefetch=1,
            grid=(MAXREQ, hops),
            in_specs=[pl.BlockSpec((1, 2, NFINE, BLOCKW), lambda q, h, a: (a[q], 0, h, 0))],
            out_specs=pl.BlockSpec((pieces, NFINE, width), lambda q, h, a: (q, h, 0)),
        ),
        cost_estimate=pl.CostEstimate(
            flops=0, transcendentals=0, bytes_accessed=MAXREQ * 8 * rows * BLOCKW
        ),
    )(arrival, incoming)


def exchange_kernel(
    owners, size, a_in, b_in, a_out, b_out, a_tmp, b_tmp, a_send, a_recv, b_send, b_recv, local
):
    column, row = lax.axis_index("chan"), lax.axis_index("tm")
    barrier = pltpu.get_barrier_semaphore()

    @pl.loop(1, owners)
    def _(step):
        other = lax.rem(column + step, owners)
        pl.semaphore_signal(barrier, inc=1, device_id={"chan": other})

    @pl.loop(1, size)
    def _(step):
        other = lax.rem(row + step, size)
        pl.semaphore_signal(barrier, inc=1, device_id={"tm": other})

    pl.semaphore_wait(barrier, owners + size - 2)

    def a_copy(step, source, target, device):
        return pltpu.make_async_remote_copy(
            src_ref=a_in.at[pl.ds(target * PAIR, PAIR)],
            dst_ref=a_out.at[pl.ds(source * PAIR, PAIR)],
            send_sem=a_send.at[step],
            recv_sem=a_recv.at[step],
            device_id={"chan": device},
        )

    def b_copy(step, source, target, device):
        return pltpu.make_async_remote_copy(
            src_ref=b_in.at[target],
            dst_ref=b_out.at[source],
            send_sem=b_send.at[step],
            recv_sem=b_recv.at[step],
            device_id={"tm": device},
        )

    @pl.loop(1, size)
    def _(step):
        target = lax.rem(row + step, size)
        b_copy(step, row, target, target).start()

    @pl.loop(1, owners)
    def _(step):
        target = lax.rem(column + step, owners)
        a_copy(step, column, target, target).start()

    a_read = pltpu.make_async_copy(a_in.at[pl.ds(column * PAIR, PAIR)], a_tmp, local.at[0])
    b_read = pltpu.make_async_copy(b_in.at[row], b_tmp, local.at[1])
    a_read.start()
    b_read.start()
    a_read.wait()
    b_read.wait()
    a_write = pltpu.make_async_copy(a_tmp, a_out.at[pl.ds(column * PAIR, PAIR)], local.at[2])
    b_write = pltpu.make_async_copy(b_tmp, b_out.at[row], local.at[3])
    a_write.start()
    b_write.start()
    a_write.wait()
    b_write.wait()

    @pl.loop(1, owners)
    def _(step):
        source = lax.rem(column + owners - step, owners)
        copy = a_copy(step, source, column, source)
        copy.wait_recv()
        copy.wait_send()

    @pl.loop(1, size)
    def _(step):
        source = lax.rem(row + size - step, size)
        copy = b_copy(step, source, row, source)
        copy.wait_recv()
        copy.wait_send()


def exchange(outgoing, sending, owners, size, collective):
    sem = pltpu.SemaphoreType.DMA
    return pl.pallas_call(
        functools.partial(exchange_kernel, owners, size),
        out_shape=(
            jax.ShapeDtypeStruct(outgoing.shape, outgoing.dtype),
            jax.ShapeDtypeStruct(sending.shape, sending.dtype),
        ),
        in_specs=[ANY, ANY],
        out_specs=(ANY, ANY),
        scratch_shapes=[
            pltpu.VMEM((PAIR,) + outgoing.shape[1:], outgoing.dtype),
            pltpu.VMEM(sending.shape[1:], sending.dtype),
            sem((owners,)),
            sem((owners,)),
            sem((size,)),
            sem((size,)),
            sem((4,)),
        ],
        compiler_params=pltpu.CompilerParams(collective_id=collective, has_side_effects=True),
    )(outgoing, sending)


def filter_kernel(hops, frames, weights_ref, *refs):
    out_ref = refs[-1]
    width = refs[0].shape[-1]

    @pl.loop(0, ROWS // STEP)
    def _(step):
        rows = pl.ds(pl.multiple_of(step * STEP, STEP), STEP)
        weights = [
            jnp.broadcast_to(weights_ref[rows, tap : tap + 1], (STEP, width)) for tap in range(TAPS)
        ]
        for frame in range(frames):
            total = None
            for tap in range(TAPS):
                hop = frame + tap
                term = weights[tap] * refs[hop % hops][hop // hops, rows, :].astype(jnp.float32)
                total = term if total is None else total + term
            out_ref[rows, frame * width : (frame + 1) * width] = total


def polyphase(parts, prototype, frames):
    hops = len(parts)
    size, _, width = parts[0].shape
    return pl.pallas_call(
        functools.partial(filter_kernel, hops, frames),
        out_shape=jax.ShapeDtypeStruct((NFINE, frames * width), jnp.float32),
        grid=(NFINE // ROWS,),
        in_specs=[pl.BlockSpec((ROWS, TAPS), lambda i: (i, 0))]
        + [pl.BlockSpec((size, ROWS, width), lambda i: (0, i, 0))] * hops,
        out_specs=pl.BlockSpec((ROWS, frames * width), lambda i: (i, 0)),
    )(prototype.T, *parts)


def combine_kernel(frames, share, both_ref, out_ref):
    frame = pl.program_id(0)

    @pl.when(frame < frames)
    def _():
        sine = both_ref[1]
        turned = jnp.concatenate([sine[:, share:], -sine[:, :share]], axis=-1)
        out_ref[0] = (both_ref[0] + turned).astype(out_ref.dtype)

    @pl.when(frame >= frames)
    def _():
        out_ref[...] = jnp.zeros_like(out_ref)


def combine(both, frames, padded, width):
    return pl.pallas_call(
        functools.partial(combine_kernel, frames, width // 2),
        out_shape=jax.ShapeDtypeStruct((padded, NFINE, width), jnp.bfloat16),
        grid=(padded,),
        in_specs=[
            pl.BlockSpec((2, NFINE, width), lambda f: (0, 0, jnp.minimum(f, frames - 1))),
        ],
        out_specs=pl.BlockSpec((1, NFINE, width), lambda f: (f, 0, 0)),
    )(both)


def return_kernel(size, keepers, hops, res_ref, out_ref, send_sems, recv_sems):
    me = lax.axis_index("tm")
    barrier = pltpu.get_barrier_semaphore()

    @pl.loop(1, size)
    def _(step):
        other = lax.rem(me + step, size)
        pl.semaphore_signal(barrier, inc=1, device_id={"tm": other})

    pl.semaphore_wait(barrier, size - 1)

    def copy(step):
        target = lax.rem(me + step, size)
        return pltpu.make_async_remote_copy(
            src_ref=res_ref.at[pl.ds(target * hops, hops)],
            dst_ref=out_ref.at[me],
            send_sem=send_sems.at[step],
            recv_sem=recv_sems.at[step],
            device_id={"tm": target},
        )

    def arriving(step):
        source = lax.rem(me + size - step, size)
        return pltpu.make_async_remote_copy(
            src_ref=res_ref.at[pl.ds(0, hops)],
            dst_ref=out_ref.at[source],
            send_sem=send_sems.at[step],
            recv_sem=recv_sems.at[step],
            device_id={"tm": source},
        )

    @pl.loop(1, size)
    def _(step):
        @pl.when(lax.rem(me + step, size) < keepers)
        def _():
            copy(step).start()

    @pl.when(me < keepers)
    def _():
        @pl.loop(1, size)
        def _(step):
            arriving(step).wait_recv()

    @pl.loop(1, size)
    def _(step):
        @pl.when(lax.rem(me + step, size) < keepers)
        def _():
            copy(step).wait_send()


def give_back(result, size, keepers, hops):
    shape = (size, hops) + result.shape[1:]
    return pl.pallas_call(
        functools.partial(return_kernel, size, keepers, hops),
        out_shape=jax.ShapeDtypeStruct(shape, result.dtype),
        in_specs=[ANY],
        out_specs=ANY,
        scratch_shapes=[pltpu.SemaphoreType.DMA((size,)), pltpu.SemaphoreType.DMA((size,))],
        compiler_params=pltpu.CompilerParams(collective_id=0, has_side_effects=True),
    )(result)


def final_kernel(pieces, meta, got_ref, own_ref, out_ref):
    share = BLOCKW // pieces
    slot, hop = pl.program_id(0), pl.program_id(1)
    row = meta[0]
    active = meta[2 + slot * pl.num_programs(1) + hop] > 0

    @pl.when(jnp.logical_not(active))
    def _():
        out_ref[...] = jnp.zeros_like(out_ref)

    @pl.when(active)
    def _():
        data = [
            jnp.where(slot * pieces + piece == row, own_ref[0], got_ref[piece, 0])
            for piece in range(pieces)
        ]
        for part in range(2):
            cols = slice(part * share, (part + 1) * share)
            out_ref[0, 0, part] = jnp.concatenate([d[:, cols] for d in data], axis=-1)


def assemble(got, result, active, row, keepers, pieces):
    size, hops, _, width = got.shape
    base = jnp.minimum(row, keepers - 1) * hops
    meta = jnp.concatenate(
        [jnp.stack([row, base]).astype(jnp.int32), active.astype(jnp.int32).reshape(-1)]
    )
    return pl.pallas_call(
        functools.partial(final_kernel, pieces),
        out_shape=jax.ShapeDtypeStruct((hops, MAXREQ, 2, NFINE, BLOCKW), got.dtype),
        grid_spec=pltpu.PrefetchScalarGridSpec(
            num_scalar_prefetch=1,
            grid=(MAXREQ, hops),
            in_specs=[
                pl.BlockSpec((pieces, 1, NFINE, width), lambda q, h, m: (q, h, 0, 0)),
                pl.BlockSpec((1, NFINE, width), lambda q, h, m: (m[1] + h, 0, 0)),
            ],
            out_specs=pl.BlockSpec((1, 1, 2, NFINE, BLOCKW), lambda q, h, m: (h, q, 0, 0, 0)),
        ),
    )(meta, got, result)


def shards(coarse, prototype, req_block, req_start, req_frames, req_count):
    owners = lax.axis_size("chan")
    column = lax.axis_index("chan")
    row = lax.axis_index("tm")
    size = lax.axis_size("tm")
    per_column = coarse.shape[2] // BLOCKW
    hops = coarse.shape[1] // NFINE
    all_hops = hops * size
    frames = all_hops - TAPS + 1
    keepers = -(-frames // hops)
    pieces = size // MAXREQ
    width = 2 * BLOCKW // pieces
    share = BLOCKW // pieces

    slot_ids = jnp.arange(MAXREQ, dtype=jnp.int32)
    live = slot_ids[None, :] < req_count[:, None]
    sources = req_block // per_column
    same = (
        live[:, :, None]
        & live[:, None, :]
        & (sources[:, :, None] == sources[:, None, :])
        & (slot_ids[None, None, :] < slot_ids[None, :, None])
    )
    rank = jnp.sum(same.astype(jnp.int32), axis=2)
    picked = (
        (live & (sources == column))[:, None, :]
        & (rank[:, None, :] == jnp.arange(PAIR, dtype=jnp.int32)[None, :, None])
    )
    local = req_block - column * per_column
    chosen = jnp.sum(jnp.where(picked, local[:, None, :], 0), axis=2).reshape(-1)
    chosen = jnp.clip(chosen, 0, per_column - 1).astype(jnp.int32)
    mine = (jnp.arange(owners, dtype=jnp.int32) == column)[:, None]

    def own(table):
        return jnp.sum(jnp.where(mine, table, 0), axis=0)

    my_live = slot_ids < own(req_count[:, None])[0]
    arrival = jnp.where(my_live, own(sources) * PAIR + own(rank), 0)
    arrival = jnp.clip(arrival, 0, owners * PAIR - 1).astype(jnp.int32)
    my_start, my_frames = own(req_start), own(req_frames)
    hop_ids = row * hops + jnp.arange(hops, dtype=jnp.int32)
    active = (
        my_live[:, None]
        & (hop_ids[None, :] >= my_start[:, None])
        & (hop_ids[None, :] < (my_start + my_frames)[:, None])
    )

    table = build_table()
    outgoing = [pack(coarse, chosen, hop, 1) for hop in range(hops)]
    incoming = lax.all_to_all(outgoing[0], "chan", split_axis=0, concat_axis=0, tiled=True)
    parts = []
    for hop in range(1, hops):
        sending = select(incoming, arrival, pieces, 1)
        incoming, gathered = exchange(outgoing[hop], sending, owners, size, hop)
        parts.append(gathered)
    sending = select(incoming, arrival, pieces, 1)
    parts.append(lax.all_to_all(sending, "tm", split_axis=0, concat_axis=0, tiled=True))
    flat = polyphase(parts, prototype, frames)
    both = jnp.dot(table, flat, precision=lax.Precision.HIGH, preferred_element_type=jnp.float32)
    padded = keepers * hops
    if width % 128 == 0:
        result = combine(both.reshape(2, NFINE, frames * width), frames, padded, width)
    else:
        both = both.reshape(2, NFINE, frames, 2, share)
        cosine, sine = both[0], both[1]
        result = jnp.stack(
            [cosine[:, :, 0] + sine[:, :, 1], cosine[:, :, 1] - sine[:, :, 0]], axis=2
        ).astype(jnp.bfloat16)
        result = result.reshape(NFINE, frames, width).transpose(1, 0, 2)
        if padded > frames:
            zeros = jnp.zeros((padded - frames, NFINE, width), result.dtype)
            result = jnp.concatenate([result, zeros], axis=0)
    got = give_back(result, size, keepers, hops)
    return assemble(got, result, active, row, keepers, pieces)[:, None]


def solution(mesh):
    return jax.shard_map(
        shards,
        mesh=mesh,
        in_specs=(P(None, "tm", "chan"), P(), P(), P(), P(), P()),
        out_specs=P("tm", "chan", None, None, None, None),
        check_vma=False,
    )
```

profile of v0, /device:TPU:7, one launch (start us, length us, event | category | flops | bytes accessed | tf_op | source)
XLA Modules:
  0.0 389.5 jit_solution(9844782129556199454)
XLA Ops:
  0.0 0.7 broadcast_subtract_fusion
  0.7 0.8 compare_and_fusion
  2.6 7.2 %shard_map.65 = bf16[8,2,1024,128]{3,2,1,0:T(8,128)(2,1)} custom-call(s32[8]{0:T(128)} %min.24.chosen, bf16[2,3072,1024]{2,1,0:T(8,128)(2,1)} %coarse_ref.5), custom_call_target="tpu_custom_call" | custom-call | bytes 8388608 | tf_op jit(solution)/shard_map/pallas_call | solution.py:35
  9.7 4.9 %all-to-all-start = ((bf16[8,2,1024,128]{3,2,1,0:T(8,128)(2,1)}), bf16[8,2,1024,128]{3,2,1,0:T(8,128)(2,1)}, u32[]{:S(2)}, u32[]{:S(2)}) async-start(bf16[8,2,1024,128]{3,2,1,0:T(8,128)(2,1)} %shard_map.65), calls=%async_computation | async-start | bytes 8388608 | tf_op jit(solution)/shard_map/all_to_all | solution.py:383
  14.7 7.2 %shard_map.68.a_in = bf16[8,2,1024,128]{3,2,1,0:T(8,128)(2,1)} custom-call(s32[8]{0:T(128)} %min.24.chosen, bf16[2,3072,1024]{2,1,0:T(8,128)(2,1)} %coarse_ref.5), custom_call_target="tpu_custom_call" | custom-call | bytes 8388608 | tf_op jit(solution)/shard_map/pallas_call | solution.py:35
  21.9 7.3 %shard_map.64.a_in = bf16[8,2,1024,128]{3,2,1,0:T(8,128)(2,1)} custom-call(s32[8]{0:T(128)} %min.24.chosen, bf16[2,3072,1024]{2,1,0:T(8,128)(2,1)} %coarse_ref.5), custom_call_target="tpu_custom_call" | custom-call | bytes 8388608 | tf_op jit(solution)/shard_map/pallas_call | solution.py:35
  29.2 0.7 select_reduce_fusion.5
  29.9 1.2 select_clamp_fusion.arrival
  31.1 30.0 %all-to-all-done.in_ref = bf16[8,2,1024,128]{3,2,1,0:T(8,128)(2,1)} async-done(((bf16[8,2,1024,128]{3,2,1,0:T(8,128)(2,1)}), bf16[8,2,1024,128]{3,2,1,0:T(8,128)(2,1)}, u32[]{:S(2)}, u32[]{:S(2)}) %all-to-all-start) | async-done | bytes 4194336 | tf_op jit(solution)/shard_map/all_to_all | solution.py:383
  61.1 4.6 %shard_map.66.b_in = bf16[8,1024,128]{2,1,0:T(8,128)(2,1)} custom-call(s32[4]{0:T(128)} %select_clamp_fusion.arrival, bf16[8,2,1024,128]{3,2,1,0:T(8,128)(2,1)} %all-to-all-done.in_ref), custom_call_target="tpu_custom_call" | custom-call | bytes 4194304 | tf_op jit(solution)/shard_map/pallas_call | solution.py:60
  65.6 50.6 %shard_map.67 = (bf16[8,2,1024,128]{3,2,1,0:T(8,128)(2,1)}, bf16[8,1024,128]{2,1,0:T(8,128)(2,1)}) custom-call(bf16[8,2,1024,128]{3,2,1,0:T(8,128)(2,1)} %shard_map.64.a_in, bf16[8,1024,128]{2,1,0:T(8,128)(2,1)} %shard_map.66.b_in), custom_call_target="tpu_custom_call" | custom-call | tf_op jit(solution)/shard_map/pallas_call | solution.py:151
  116.3 4.6 %shard_map.69.b_in = bf16[8,1024,128]{2,1,0:T(8,128)(2,1)} custom-call(s32[4]{0:T(128)} %select_clamp_fusion.arrival, bf16[8,2,1024,128]{3,2,1,0:T(8,128)(2,1)} %get-tuple-element.10.in_ref), custom_call_target="tpu_custom_call" | custom-call | bytes 4194304 | tf_op jit(solution)/shard_map/pallas_call | solution.py:60
  120.8 49.5 %shard_map.70 = (bf16[8,2,1024,128]{3,2,1,0:T(8,128)(2,1)}, bf16[8,1024,128]{2,1,0:T(8,128)(2,1)}) custom-call(bf16[8,2,1024,128]{3,2,1,0:T(8,128)(2,1)} %shard_map.68.a_in, bf16[8,1024,128]{2,1,0:T(8,128)(2,1)} %shard_map.69.b_in), custom_call_target="tpu_custom_call" | custom-call | tf_op jit(solution)/shard_map/pallas_call | solution.py:151
  170.4 4.7 %shard_map.71 = bf16[8,1024,128]{2,1,0:T(8,128)(2,1)} custom-call(s32[4]{0:T(128)} %select_clamp_fusion.arrival, bf16[8,2,1024,128]{3,2,1,0:T(8,128)(2,1)} %get-tuple-element.12.in_ref), custom_call_target="tpu_custom_call" | custom-call | bytes 4194304 | tf_op jit(solution)/shard_map/pallas_call | solution.py:60
  175.1 4.7 %all-to-all-start.1 = ((bf16[8,1024,128]{2,1,0:T(8,128)(2,1)}), bf16[8,1024,128]{2,1,0:T(8,128)(2,1)S(1)}, u32[]{:S(2)}, u32[]{:S(2)}) async-start(bf16[8,1024,128]{2,1,0:T(8,128)(2,1)} %shard_map.71), calls=%async_computation.1 | async-start | bytes 4194304 | tf_op jit(solution)/shard_map/all_to_all | solution.py:390
  180.6 1.0 copy.11
  182.3 17.8 %sine_multiply_fusion = (f32[1024,1024]{1,0:T(8,128)}, f32[1024,1024]{1,0:T(8,128)}) fusion(), kind=kLoop, calls=%fused_computation.10 | loop fusion | flops 16777216 | bytes 8388608 | tf_op jit(solution)/shard_map/mul | solution.py:26
  200.1 27.3 %all-to-all-done.1.refs_2_ = bf16[8,1024,128]{2,1,0:T(8,128)(2,1)S(1)} async-done(((bf16[8,1024,128]{2,1,0:T(8,128)(2,1)}), bf16[8,1024,128]{2,1,0:T(8,128)(2,1)S(1)}, u32[]{:S(2)}, u32[]{:S(2)}) %all-to-all-start.1) | async-done | bytes 2097184 | tf_op jit(solution)/shard_map/all_to_all | solution.py:390
  227.3 1.3 copy-done
  228.7 12.1 %shard_map.72 = f32[1024,1152]{1,0:T(8,128)} custom-call(f32[1024,16]{1,0:T(8,128)} %bitcast.9, bf16[8,1024,128]{2,1,0:T(8,128)(2,1)} %get-tuple-element.9.refs_0_, bf16[8,1024,128]{2,1,0:T(8,128)(2,1)} %get-tuple-element.11.refs_1_, bf16[8,1024,128]{2,1,0:T(8,128)(2,1)} %copy-done), custom_call_target="tpu_custom_call" | custom-call | tf_op jit(solution)/shard_map/pallas_call | solution.py:194
  240.7 22.6 %fusion = f32[2048,1152]{1,0:T(8,128)} fusion(f32[1024,1152]{1,0:T(8,128)} %shard_map.72, f32[1024,1024]{1,0:T(8,128)} %get-tuple-element.21, f32[1024,1024]{1,0:T(8,128)} %get-tuple-element.22), kind=kOutput, calls=%fused_computation | convolution fusion | flops 14497611776 | bytes 22544384 | tf_op jit(solution)/shard_map/dot_general | solution.py:392
  263.3 9.2 %shard_map.73.res_ref.own_ref = bf16[9,1024,128]{2,1,0:T(8,128)(2,1)} custom-call(f32[2,1024,1152]{2,1,0:T(8,128)} %bitcast.8), custom_call_target="tpu_custom_call" | custom-call | tf_op jit(solution)/shard_map/pallas_call | solution.py:219
  272.6 106.0 %shard_map.74.got_ref = bf16[8,3,1024,128]{3,2,1,0:T(8,128)(2,1)} custom-call(bf16[9,1024,128]{2,1,0:T(8,128)(2,1)} %shard_map.73.res_ref.own_ref), custom_call_target="tpu_custom_call" | custom-call | tf_op jit(solution)/shard_map/pallas_call | solution.py:282
  378.6 10.9 %shard_map.75 = bf16[3,4,2,1024,128]{4,3,2,1,0:T(8,128)(2,1)} custom-call(s32[14]{0:T(128)} %pad_add_fusion.meta, bf16[8,3,1024,128]{3,2,1,0:T(8,128)(2,1)} %shard_map.74.got_ref, bf16[9,1024,128]{2,1,0:T(8,128)(2,1)} %shard_map.73.res_ref.own_ref), custom_call_target="tpu_custom_call" | custom-call | tf_op jit(solution)/shard_map/pallas_call | solution.py:319
  (22 shorter events, 2.6 us)
Async XLA Ops:
  9.7 51.3 %all-to-all-start = ((bf16[8,2,1024,128]{3,2,1,0:T(8,128)(2,1)}), bf16[8,2,1024,128]{3,2,1,0:T(8,128)(2,1)}, u32[]{:S(2)}, u32[]{:S(2)}) async-start(bf16[8,2,1024,128]{3,2,1,0:T(8,128)(2,1)} %shard_map.65), calls=%async_computation | async-start | bytes 8388608 | tf_op jit(solution)/shard_map/all_to_all | solution.py:383
  21.8 7.3 %copy-start.4 = (s32[4]{0:T(128)S(1)}, s32[4]{0:T(128)}, u32[]{:S(2)}) copy-start(s32[4]{0:T(128)} %param.11) | copy-start | bytes 52
  21.8 8.0 %copy-start.2 = (s32[4,4]{1,0:T(4,128)S(1)}, s32[4,4]{1,0:T(4,128)}, u32[]{:S(2)}) copy-start(s32[4,4]{1,0:T(4,128)} %param.9) | copy-start | bytes 196
  21.9 8.0 %copy-start.3 = (s32[4,4]{1,0:T(4,128)S(1)}, s32[4,4]{1,0:T(4,128)}, u32[]{:S(2)}) copy-start(s32[4,4]{1,0:T(4,128)} %param.10) | copy-start | bytes 196
  170.4 10.2 %copy-start.1 = (f32[16,1024]{1,0:T(8,128)S(1)}, f32[16,1024]{1,0:T(8,128)}, u32[]{:S(2)}) copy-start(f32[16,1024]{1,0:T(8,128)} %param.7) | copy-start | bytes 196612
  175.1 52.2 %all-to-all-start.1 = ((bf16[8,1024,128]{2,1,0:T(8,128)(2,1)}), bf16[8,1024,128]{2,1,0:T(8,128)(2,1)S(1)}, u32[]{:S(2)}, u32[]{:S(2)}) async-start(bf16[8,1024,128]{2,1,0:T(8,128)(2,1)} %shard_map.71), calls=%async_computation.1 | async-start | bytes 4194304 | tf_op jit(solution)/shard_map/all_to_all | solution.py:390
  227.3 1.4 copy-start
where the time goes:
time: 392 us; the launch traced here: 389 us
  Pallas kernels  274 us (70%)
  waiting for transfers between devices  57.2 us (15%)
  other arithmetic  22.9 us (6%)
  matrix products  22.6 us (6%)
  starting transfers between devices  9.65 us (2%)
    pallas_call x1, Pallas kernels, give_back(): pl.pallas_call(functools.partial(return_kernel, size, keepers, hops), out...  106 us
    pallas_call x2, Pallas kernels, exchange(): pl.pallas_call(functools.partial(exchange_kernel, owners, size), out_shap...  100 us
    all_to_all x1, waiting for transfers between devices, shards(): lax.all_to_all(outgoing[0], 'chan', split_axis=0, concat_axis=0, tiled=True)  30 us
    all_to_all x1, waiting for transfers between devices, shards(): lax.all_to_all(sending, 'tm', split_axis=0, concat_axis=0, tiled=True)  27.3 us
    dot_general x1, matrix products, shards(): jnp.dot(table, flat, precision=lax.Precision.HIGH, preferred_element_type...  22.6 us
    pallas_call x3, Pallas kernels, pack(): pl.pallas_call(pack_kernel, out_shape=jax.ShapeDtypeStruct((count, 2, hop...  21.6 us
    mul x1, other arithmetic, build_table(): jnp.sin(angles) * scale  17.8 us
    pallas_call x3, Pallas kernels, select(): pl.pallas_call(functools.partial(select_kernel, pieces), out_shape=jax.Sh...  13.9 us
  transfers between devices with their start and end apart: 2, of which 2 were waited for; matrix products, arithmetic and copies ran while one was open for 6% of the time, Pallas kernels for 4%

commit v1 on v0

--- a/solution.py
+++ b/solution.py
@@ -3,6 +3,7 @@
 
 import jax
 import jax.numpy as jnp
+import numpy as np
 from jax import lax
 from jax.experimental import pallas as pl
 from jax.experimental.pallas import tpu as pltpu
@@ -331,7 +332,7 @@
     )(meta, got, result)
 
 
-def shards(coarse, prototype, req_block, req_start, req_frames, req_count):
+def shards_general(coarse, prototype, req_block, req_start, req_frames, req_count):
     owners = lax.axis_size("chan")
     column = lax.axis_index("chan")
     row = lax.axis_index("tm")
@@ -407,6 +408,611 @@
     return assemble(got, result, active, row, keepers, pieces)[:, None]
 
 
+SMEM = pl.BlockSpec(memory_space=pltpu.SMEM)
+TOP = 32767.0
+RADIX = 4
+SUB = NFINE // RADIX
+
+
+def round_up(value, unit):
+    return -(-value // unit) * unit
+
+
+def tables_kernel(plan, blk, start, nfr, cnt, meta, chosen, reqs, pos, omap, columns, lists):
+    row, col = lax.axis_index("tm"), lax.axis_index("chan")
+    for i in range(plan.owners):
+        columns[i] = 0
+    for i in range(plan.keepers * plan.owners):
+        lists[i] = 0
+    for i in range(plan.hops * MAXREQ):
+        omap[i] = -1
+    for i in range(plan.fill):
+        chosen[i] = 0
+
+    def request(index, carry):
+        owner, slot = lax.div(index, MAXREQ), lax.rem(index, MAXREQ)
+
+        def add(carry):
+            count, units = carry
+            block = blk[owner, slot]
+            source = lax.div(block, plan.per_column)
+            place = columns[source]
+            columns[source] = place + 1
+            first = start[owner, slot]
+            last = first + nfr[owner, slot]
+            reqs[0, count] = source
+            reqs[1, count] = place
+            reqs[2, count] = first
+            reqs[3, count] = last
+            reqs[4, count] = units
+
+            @pl.when(source == col)
+            def _():
+                chosen[place] = block - source * plan.per_column
+
+            def frame(hop, carry):
+                keeper = lax.div(hop, plan.hops)
+                line = keeper * plan.owners + owner
+                entry = lists[line]
+                lists[line] = entry + 1
+                pos[count * plan.frames + hop] = line * plan.deep + entry
+
+                @pl.when((keeper == row) & (owner == col))
+                def _():
+                    omap[(hop - keeper * plan.hops) * MAXREQ + slot] = entry
+
+                return carry
+
+            lax.fori_loop(first, last, frame, 0)
+            return count + 1, units + last - first
+
+        return lax.cond(slot < cnt[owner], add, lambda carry: carry, carry)
+
+    count, units = lax.fori_loop(
+        0, plan.owners * MAXREQ, request, (jnp.int32(0), jnp.int32(0))
+    )
+    longest, deepest = jnp.int32(0), jnp.int32(0)
+    for i in range(plan.owners):
+        longest = jnp.maximum(longest, columns[i])
+    for i in range(plan.keepers * plan.owners):
+        deepest = jnp.maximum(deepest, lists[i])
+    meta[0] = columns[col]
+    meta[1] = count
+    meta[2] = longest
+    meta[3] = units
+    meta[4] = deepest
+    meta[5] = row
+
+
+def make_tables(plan, req_block, req_start, req_frames, req_count):
+    total = plan.owners * MAXREQ
+    shape = lambda *dims: jax.ShapeDtypeStruct(dims, jnp.int32)
+    return pl.pallas_call(
+        functools.partial(tables_kernel, plan),
+        out_shape=(
+            shape(8),
+            shape(plan.fill),
+            shape(5, total),
+            shape(total * plan.frames),
+            shape(plan.hops * MAXREQ),
+        ),
+        in_specs=[SMEM] * 4,
+        out_specs=(SMEM,) * 5,
+        scratch_shapes=[
+            pltpu.SMEM((plan.owners,), jnp.int32),
+            pltpu.SMEM((plan.keepers * plan.owners,), jnp.int32),
+        ],
+    )(req_block, req_start, req_frames, req_count)
+
+
+def gather_kernel(plan, meta, chosen, in_ref, out_ref):
+    @pl.when(pl.program_id(1) < jnp.maximum(meta[0], 1))
+    def _():
+        for piece in range(plan.slices):
+            out_ref[piece, 0, 0] = in_ref[:, piece * plan.span : (piece + 1) * plan.span, :]
+
+
+def gather(plan, coarse, meta, chosen):
+    def place(i, m):
+        return jnp.minimum(i, jnp.maximum(m[0] - 1, 0))
+
+    return pl.pallas_call(
+        functools.partial(gather_kernel, plan),
+        out_shape=jax.ShapeDtypeStruct(
+            (plan.slices, plan.fill, plan.hops, 2, plan.span, BLOCKW), coarse.dtype
+        ),
+        grid_spec=pltpu.PrefetchScalarGridSpec(
+            num_scalar_prefetch=2,
+            grid=(plan.hops, plan.fill),
+            in_specs=[
+                pl.BlockSpec((2, NFINE, BLOCKW), lambda h, i, m, c: (0, h, c[place(i, m)]))
+            ],
+            out_specs=pl.BlockSpec(
+                (plan.slices, 1, 1, 2, plan.span, BLOCKW),
+                lambda h, i, m, c: (0, place(i, m), h, 0, 0, 0),
+            ),
+        ),
+    )(meta, chosen, coarse)
+
+
+def spread_kernel(plan, count, src, dst, tmp, send, recv, local):
+    row, col = lax.axis_index("tm"), lax.axis_index("chan")
+    size = plan.slices
+    base = lax.div(row, plan.half) * plan.half
+    me = (row - base) * plan.owners + col
+    barrier = pltpu.get_barrier_semaphore()
+
+    def device(index):
+        return {"tm": base + lax.div(index, plan.owners), "chan": lax.rem(index, plan.owners)}
+
+    order = plan.masks
+
+    for mask in order:
+        pl.semaphore_signal(barrier, inc=1, device_id=device(me ^ mask))
+    pl.semaphore_wait(barrier, len(order))
+
+    def copy(place, mask, source, target):
+        return pltpu.make_async_remote_copy(
+            src_ref=src.at[target, place],
+            dst_ref=dst.at[source, place],
+            send_sem=send.at[place, mask],
+            recv_sem=recv.at[place, mask],
+            device_id=device(me ^ mask),
+        )
+
+    @pl.loop(0, count)
+    def _(place):
+        for mask in order:
+            copy(place, mask, me, me ^ mask).start()
+
+    read = pltpu.make_async_copy(src.at[me, pl.ds(0, count)], tmp, local.at[0])
+    read.start()
+    read.wait()
+    write = pltpu.make_async_copy(tmp, dst.at[me, pl.ds(0, count)], local.at[1])
+    write.start()
+    write.wait()
+
+    @pl.loop(0, count)
+    def _(place):
+        for mask in order:
+            copy(place, mask, me ^ mask, me).wait_recv()
+            copy(place, mask, me, me ^ mask).wait_send()
+
+
+def spread(plan, packed, count, collective):
+    sem = pltpu.SemaphoreType.DMA
+    return pl.pallas_call(
+        functools.partial(spread_kernel, plan, count),
+        out_shape=jax.ShapeDtypeStruct(packed.shape, packed.dtype),
+        in_specs=[ANY],
+        out_specs=ANY,
+        scratch_shapes=[
+            pltpu.VMEM((count,) + packed.shape[2:], packed.dtype),
+            sem((count, plan.slices)),
+            sem((count, plan.slices)),
+            sem((2,)),
+        ],
+        compiler_params=pltpu.CompilerParams(collective_id=collective, has_side_effects=True),
+    )(packed)
+
+
+def partial_sum(plan, upper, hop, w_ref, in_ref, part):
+    first = (plan.half * plan.hops if upper else 0) + plan.frames - 1
+    total = None
+    for index in range(plan.half * plan.hops):
+        source, local = divmod(index, plan.hops)
+        term = w_ref[first + index - hop] * in_ref[source, 0, 0, local, part].astype(jnp.float32)
+        total = term if total is None else total + term
+    return total
+
+
+def encode(parts, out_ref, scale_ref, place, scale_row):
+    top = jnp.max(jnp.maximum(jnp.abs(parts[0]), jnp.abs(parts[1])), axis=0, keepdims=True)
+    top = jnp.maximum(top, 1e-30)
+    factor = TOP / top
+    for part in range(2):
+        code = jnp.round(parts[part] * factor).astype(jnp.int32)
+        out_ref[place, part] = code.astype(jnp.int16)
+    scale_ref[pl.ds(scale_row, 1), :] = top * (1.0 / TOP)
+
+
+def upper_kernel(plan, meta, reqs, in_ref, w_ref, out_ref, scale_ref):
+    index = pl.program_id(0)
+
+    @pl.when((index < meta[1]) & (meta[5] >= plan.half))
+    def _():
+        first, last, offset = reqs[2, index], reqs[3, index], reqs[4, index]
+
+        @pl.loop(first, last)
+        def _(hop):
+            parts = [partial_sum(plan, True, hop, w_ref, in_ref, part) for part in range(2)]
+            place = offset + hop - first
+            encode(parts, out_ref, scale_ref, place, place)
+
+
+def lower_kernel(plan, meta, reqs, pos, in_ref, w_ref, got_ref, got_scale, out_ref, scale_ref):
+    index = pl.program_id(0)
+
+    @pl.when((index < meta[1]) & (meta[5] < plan.half))
+    def _():
+        first, last, offset = reqs[2, index], reqs[3, index], reqs[4, index]
+
+        @pl.loop(first, last)
+        def _(hop):
+            unit = offset + hop - first
+            scale = got_scale[pl.ds(unit, 1), :]
+            parts = []
+            for part in range(2):
+                other = got_ref[unit, part].astype(jnp.int32).astype(jnp.float32) * scale
+                parts.append(partial_sum(plan, False, hop, w_ref, in_ref, part) + other)
+            place = pos[index * plan.frames + hop]
+            encode(parts, out_ref, scale_ref, place, place)
+
+
+def filter_specs(plan):
+    def request(i, m):
+        return jnp.minimum(i, jnp.maximum(m[1] - 1, 0))
+
+    taps = plan.frames - 1 + plan.all_hops
+    return [
+        pl.BlockSpec(
+            (plan.half, 1, 1, plan.hops, 2, plan.span, BLOCKW),
+            lambda i, m, r, *_: (0, r[0, request(i, m)], r[1, request(i, m)], 0, 0, 0, 0),
+        ),
+        pl.BlockSpec((taps, plan.span, BLOCKW), lambda i, *_: (0, 0, 0)),
+    ]
+
+
+def whole(*dims):
+    return pl.BlockSpec(dims, lambda i, *_: (0,) * len(dims))
+
+
+def filter_upper(plan, spreaded, weights, meta, reqs):
+    units = plan.units
+    return pl.pallas_call(
+        functools.partial(upper_kernel, plan),
+        out_shape=(
+            jax.ShapeDtypeStruct((units, 2, plan.span, BLOCKW), jnp.int16),
+            jax.ShapeDtypeStruct((units, BLOCKW), jnp.float32),
+        ),
+        grid_spec=pltpu.PrefetchScalarGridSpec(
+            num_scalar_prefetch=2,
+            grid=(plan.owners * MAXREQ,),
+            in_specs=filter_specs(plan),
+            out_specs=(whole(units, 2, plan.span, BLOCKW), whole(units, BLOCKW)),
+        ),
+    )(meta, reqs, spreaded, weights)
+
+
+def filter_lower(plan, spreaded, weights, got, scales, meta, reqs, pos):
+    units = plan.units
+    rows = plan.keepers * plan.owners * plan.deep
+    return pl.pallas_call(
+        functools.partial(lower_kernel, plan),
+        out_shape=(
+            jax.ShapeDtypeStruct((rows, 2, plan.span, BLOCKW), jnp.int16),
+            jax.ShapeDtypeStruct((rows, BLOCKW), jnp.float32),
+        ),
+        grid_spec=pltpu.PrefetchScalarGridSpec(
+            num_scalar_prefetch=3,
+            grid=(plan.owners * MAXREQ,),
+            in_specs=filter_specs(plan)
+            + [whole(units, 2, plan.span, BLOCKW), whole(units, BLOCKW)],
+            out_specs=(whole(rows, 2, plan.span, BLOCKW), whole(rows, BLOCKW)),
+        ),
+    )(meta, reqs, pos, spreaded, weights, got, scales)
+
+
+def lift_kernel(plan, count, src, src_scale, dst, dst_scale, send, recv):
+    row = lax.axis_index("tm")
+    barrier = pltpu.get_barrier_semaphore()
+    upper = row >= plan.half
+    other = jnp.where(upper, row - plan.half, row + plan.half)
+    pl.semaphore_signal(barrier, inc=1, device_id={"tm": other})
+    pl.semaphore_wait(barrier, 1)
+    refs = [(src, dst), (src_scale, dst_scale)]
+    copies = [
+        pltpu.make_async_remote_copy(
+            src_ref=source.at[pl.ds(0, count)],
+            dst_ref=target.at[pl.ds(0, count)],
+            send_sem=send.at[index],
+            recv_sem=recv.at[index],
+            device_id={"tm": other},
+        )
+        for index, (source, target) in enumerate(refs)
+    ]
+
+    @pl.when(upper)
+    def _():
+        for copy in copies:
+            copy.start()
+        for copy in copies:
+            copy.wait_send()
+
+    @pl.when(jnp.logical_not(upper))
+    def _():
+        for copy in copies:
+            copy.wait_recv()
+
+
+def lift(plan, values, scales, count, collective):
+    sem = pltpu.SemaphoreType.DMA
+    return pl.pallas_call(
+        functools.partial(lift_kernel, plan, count),
+        out_shape=(
+            jax.ShapeDtypeStruct(values.shape, values.dtype),
+            jax.ShapeDtypeStruct(scales.shape, scales.dtype),
+        ),
+        in_specs=[ANY, ANY],
+        out_specs=(ANY, ANY),
+        scratch_shapes=[sem((2,)), sem((2,))],
+        compiler_params=pltpu.CompilerParams(collective_id=collective, has_side_effects=True),
+    )(values, scales)
+
+
+def deliver_kernel(plan, count, src, src_scale, dst, dst_scale, tmp, tmp_scale, send, recv, local):
+    row, col = lax.axis_index("tm"), lax.axis_index("chan")
+    size, lines = plan.slices, plan.keepers * plan.owners
+    me = row * plan.owners + col
+    barrier = pltpu.get_barrier_semaphore()
+
+    def device(index):
+        return {"tm": lax.div(index, plan.owners), "chan": lax.rem(index, plan.owners)}
+
+    def copies(step, source, target, other):
+        values = pltpu.make_async_remote_copy(
+            src_ref=src.at[target, pl.ds(0, count)],
+            dst_ref=dst.at[source, pl.ds(0, count)],
+            send_sem=send.at[0, step],
+            recv_sem=recv.at[0, step],
+            device_id=device(other),
+        )
+        scales = pltpu.make_async_remote_copy(
+            src_ref=src_scale.at[target],
+            dst_ref=dst_scale.at[source],
+            send_sem=send.at[1, step],
+            recv_sem=recv.at[1, step],
+            device_id=device(other),
+        )
+        return values, scales
+
+    @pl.when(row < plan.half)
+    def _():
+        @pl.loop(1, size)
+        def _(step):
+            pl.semaphore_signal(barrier, inc=1, device_id=device(lax.rem(me + step, size)))
+
+        pl.semaphore_wait(barrier, size - 1)
+
+        @pl.loop(1, size)
+        def _(step):
+            target = lax.rem(me + step, size)
+
+            @pl.when(target < lines)
+            def _():
+                for copy in copies(step, me, target, target):
+                    copy.start()
+
+        @pl.when(me < lines)
+        def _():
+            moves = [
+                (src.at[me, pl.ds(0, count)], tmp, dst.at[me, pl.ds(0, count)]),
+                (src_scale.at[me], tmp_scale, dst_scale.at[me]),
+            ]
+            for index, (source, middle, target) in enumerate(moves):
+                read = pltpu.make_async_copy(source, middle, local.at[2 * index])
+                read.start()
+                read.wait()
+                write = pltpu.make_async_copy(middle, target, local.at[2 * index + 1])
+                write.start()
+                write.wait()
+
+            @pl.loop(1, size)
+            def _(step):
+                source = lax.rem(me + size - step, size)
+                for copy in copies(step, source, me, source):
+                    copy.wait_recv()
+
+        @pl.loop(1, size)
+        def _(step):
+            target = lax.rem(me + step, size)
+
+            @pl.when(target < lines)
+            def _():
+                for copy in copies(step, me, target, target):
+                    copy.wait_send()
+
+
+def deliver(plan, values, scales, count, collective):
+    sem = pltpu.SemaphoreType.DMA
+    inner = values.shape[1:]
+    return pl.pallas_call(
+        functools.partial(deliver_kernel, plan, count),
+        out_shape=(
+            jax.ShapeDtypeStruct((plan.slices,) + inner, values.dtype),
+            jax.ShapeDtypeStruct((plan.slices,) + scales.shape[1:], scales.dtype),
+        ),
+        in_specs=[ANY, ANY],
+        out_specs=(ANY, ANY),
+        scratch_shapes=[
+            pltpu.VMEM((count,) + inner[1:], values.dtype),
+            pltpu.VMEM(scales.shape[1:], scales.dtype),
+            sem((2, plan.slices)),
+            sem((2, plan.slices)),
+            sem((4,)),
+        ],
+        compiler_params=pltpu.CompilerParams(collective_id=collective, has_side_effects=True),
+    )(values, scales)
+
+
+def transform_kernel(plan, omap, in_ref, scale_ref, high_ref, low_ref, turn_ref, out_ref, yh, yl, zs):
+    entry = omap[pl.program_id(0)]
+
+    @pl.when(entry < 0)
+    def _():
+        out_ref[...] = jnp.zeros_like(out_ref)
+
+    @pl.when(entry >= 0)
+    def _():
+        chunk = 32
+
+        def load(part, first):
+            piece, line = divmod(first, plan.span)
+            code = in_ref[piece, 0, part, line : line + chunk, :]
+            scale = scale_ref[piece, pl.ds(entry, 1), :]
+            return code.astype(jnp.int32).astype(jnp.float32) * scale
+
+        for line in range(0, SUB, chunk):
+            re = [load(0, SUB * a + line) for a in range(RADIX)]
+            im = [load(1, SUB * a + line) for a in range(RADIX)]
+            es, ed = re[0] + re[2], re[0] - re[2]
+            fs, fd = im[0] + im[2], im[0] - im[2]
+            gs, gd = re[1] + re[3], re[1] - re[3]
+            hs, hd = im[1] + im[3], im[1] - im[3]
+            mixed = [
+                (es + gs, fs + hs),
+                (ed + hd, fd - gd),
+                (es - gs, fs - hs),
+                (ed - hd, fd + gd),
+            ]
+            rows = slice(line, line + chunk)
+            for q in range(RADIX):
+                real, imag = mixed[q]
+                if q:
+                    cosine, sine = turn_ref[0, q - 1, rows, :], turn_ref[1, q - 1, rows, :]
+                    real, imag = real * cosine + imag * sine, imag * cosine - real * sine
+                for part, value in enumerate((real, imag)):
+                    cols = slice(part * BLOCKW, (part + 1) * BLOCKW)
+                    high = value.astype(jnp.bfloat16)
+                    yh[q, rows, cols] = high
+                    yl[q, rows, cols] = (value - high.astype(jnp.float32)).astype(jnp.bfloat16)
+
+        for q in range(RADIX):
+            both = jnp.dot(high_ref[...], yh[q], preferred_element_type=jnp.float32)
+            both = both + jnp.dot(high_ref[...], yl[q], preferred_element_type=jnp.float32)
+            both = both + jnp.dot(low_ref[...], yh[q], preferred_element_type=jnp.float32)
+            rows = pl.ds(q, SUB, stride=RADIX)
+            zs[0, rows, :] = both[:SUB, :BLOCKW] + both[SUB:, BLOCKW:]
+            zs[1, rows, :] = both[:SUB, BLOCKW:] - both[SUB:, :BLOCKW]
+
+        out_ref[0, 0] = zs[...].astype(out_ref.dtype)
+
+
+def transform_tables():
+    line = np.arange(SUB)
+    angles = (line[:, None] * line[None, :] % SUB) * (2.0 * np.pi / SUB)
+    table = np.concatenate([np.cos(angles), np.sin(angles)], axis=0) / math.sqrt(NFINE)
+    table = table.astype(np.float32)
+    high = table.astype(jnp.bfloat16)
+    low = (table - high.astype(np.float32)).astype(jnp.bfloat16)
+    turns = np.arange(1, RADIX)[:, None] * line[None, :] * (2.0 * np.pi / NFINE)
+    turn = np.stack([np.cos(turns), np.sin(turns)]).astype(np.float32)
+    return high, low, turn
+
+
+def transform(plan, values, scales, omap):
+    high, low, turn = transform_tables()
+    turn = jnp.broadcast_to(jnp.asarray(turn)[..., None], turn.shape + (BLOCKW,))
+    return pl.pallas_call(
+        functools.partial(transform_kernel, plan),
+        out_shape=jax.ShapeDtypeStruct((plan.hops, MAXREQ, 2, NFINE, BLOCKW), jnp.bfloat16),
+        grid_spec=pltpu.PrefetchScalarGridSpec(
+            num_scalar_prefetch=1,
+            grid=(plan.hops * MAXREQ,),
+            in_specs=[
+                pl.BlockSpec(
+                    (plan.slices, 1, 2, plan.span, BLOCKW),
+                    lambda i, o: (0, jnp.maximum(o[i], 0), 0, 0, 0),
+                ),
+                whole(*scales.shape),
+                whole(2 * SUB, SUB),
+                whole(2 * SUB, SUB),
+                whole(2, RADIX - 1, SUB, BLOCKW),
+            ],
+            out_specs=pl.BlockSpec(
+                (1, 1, 2, NFINE, BLOCKW), lambda i, o: (i // MAXREQ, i % MAXREQ, 0, 0, 0)
+            ),
+            scratch_shapes=[
+                pltpu.VMEM((RADIX, SUB, 2 * BLOCKW), jnp.bfloat16),
+                pltpu.VMEM((RADIX, SUB, 2 * BLOCKW), jnp.bfloat16),
+                pltpu.VMEM((2, NFINE, BLOCKW), jnp.float32),
+            ],
+        ),
+    )(omap, values, scales, jnp.asarray(high), jnp.asarray(low), turn)
+
+
+def owners_power(value):
+    return value & (value - 1) == 0
+
+
+class Plan:
+    def __init__(self, size, owners, hops, per_column):
+        self.size, self.owners, self.hops, self.per_column = size, owners, hops, per_column
+        self.all_hops = hops * size
+        self.frames = self.all_hops - TAPS + 1
+        self.keepers = -(-self.frames // hops)
+        self.half = size // 2
+        self.slices = self.half * owners
+        self.span = NFINE // self.slices
+        self.fill = owners * PAIR
+        self.deep = round_up(hops * MAXREQ, 8)
+        self.units = round_up(owners * MAXREQ * self.frames, 16)
+
+        spread = sorted(range(2, self.slices), key=lambda mask: bin(mask >> 1).count("1"))
+        self.masks = spread + [1]
+
+    def fits(self):
+        powers = self.slices & (self.slices - 1) == 0 and owners_power(self.owners)
+        even = powers and self.size % 2 == 0 and NFINE % self.slices == 0 and self.span % 32 == 0
+        return even and self.keepers <= self.half
+
+
+def choose(value, sizes, build, first, *operands):
+    index = sum((value > size).astype(jnp.int32) for size in sizes[:-1])
+    branches = [functools.partial(build, size, first + i) for i, size in enumerate(sizes)]
+    return lax.switch(index, branches, *operands)
+
+
+def shards(coarse, prototype, req_block, req_start, req_frames, req_count):
+    owners, size = lax.axis_size("chan"), lax.axis_size("tm")
+    plan = Plan(size, owners, coarse.shape[1] // NFINE, coarse.shape[2] // BLOCKW)
+    if not plan.fits():
+        return shards_general(coarse, prototype, req_block, req_start, req_frames, req_count)
+    meta, chosen, reqs, pos, omap = make_tables(plan, req_block, req_start, req_frames, req_count)
+    packed = gather(plan, coarse, meta, chosen)
+
+    me = lax.axis_index("tm") % plan.half * owners + lax.axis_index("chan")
+    mine = lax.dynamic_slice(prototype, (0, me * plan.span), (TAPS, plan.span))
+    mine = jnp.pad(mine, ((plan.frames - 1, plan.all_hops - TAPS), (0, 0)))
+    weights = jnp.broadcast_to(mine[:, :, None], mine.shape + (BLOCKW,))
+
+    fills = sorted({max(1, plan.fill * i // 8) for i in (2, 3, 4, 5, 6, 8)})
+    spreaded = choose(
+        meta[2], fills, lambda n, c, x: spread(plan, x, n, c), 0, packed
+    )
+    spreaded = spreaded.reshape((plan.half, owners) + spreaded.shape[1:])
+    values, scales = filter_upper(plan, spreaded, weights, meta, reqs)
+    counts = sorted({round_up(plan.units * i // 9, 16) for i in (2, 3, 4, 5, 6, 9)})
+    values, scales = choose(
+        meta[3], counts, lambda n, c, *x: lift(plan, *x, n, c), len(fills), values, scales
+    )
+    values, scales = filter_lower(plan, spreaded, weights, values, scales, meta, reqs, pos)
+    lines = plan.keepers * owners
+    values = values.reshape((lines, plan.deep) + values.shape[1:])
+    scales = scales.reshape((lines, plan.deep) + scales.shape[1:])
+    most = plan.hops * MAXREQ
+    depths = sorted({-(-most * i // 12) for i in (6, 7, 8, 9, 10, 12)})
+    values, scales = choose(
+        meta[4],
+        depths,
+        lambda n, c, *x: deliver(plan, *x, n, c),
+        len(fills) + len(counts),
+        values,
+        scales,
+    )
+    return transform(plan, values, scales, omap)[:, None]
+
+
 def solution(mesh):
     return jax.shard_map(
         shards,

time: 392 us -> 357 us (0.911); the launches traced: 389 us -> 360 us
  Pallas kernels: 274 us -> 347 us
  waiting for transfers between devices: 57.2 us -> 0 us
  other arithmetic: 22.9 us -> 0 us
  matrix products: 22.6 us -> 0 us
  starting transfers between devices: 9.65 us -> 0 us
  between operations: 0.08 us -> 9.23 us
    pallas_call x12 -> x8, Pallas kernels: 274 us -> 347 us  [the longest x1 126 us: spread(): pl.pallas_call(functools.partial(spread_kernel, plan, count), out_shape=j...]
    all_to_all x2 -> x0, waiting for transfers between devices: 57.2 us -> none  [the longest x1 30 us: shards(): lax.all_to_all(outgoing[0], 'chan', split_axis=0, concat_axis=0, tiled=True)]
    dot_general x1 -> x0, matrix products: 22.6 us -> none  [shards(): jnp.dot(table, flat, precision=lax.Precision.HIGH, preferred_element_type...]
    mul x1 -> x0, other arithmetic: 17.8 us -> none  [build_table(): jnp.sin(angles) * scale]
    all_to_all x2 -> x0, starting transfers between devices: 9.65 us -> none  [the longest x1 4.95 us: shards(): lax.all_to_all(outgoing[0], 'chan', split_axis=0, concat_axis=0, tiled=True)]
  transfers between devices with their start and end apart: 2 -> 0, of which waited for: 2 -> 0; matrix products, arithmetic and copies ran while one was open for 6% -> 0% of each run, Pallas kernels for 4% -> 0%
where the time goes in v1:
time: 357 us; the launch traced here: 360 us
  Pallas kernels  347 us (97%)
  between operations  9.23 us (3%)
  local copies, waits for them, and re-layouts  4.04 us (1%)
    pallas_call x1, Pallas kernels, spread(): pl.pallas_call(functools.partial(spread_kernel, plan, count), out_shape=j...  126 us
    pallas_call x1, Pallas kernels, lift(): pl.pallas_call(functools.partial(lift_kernel, plan, count), out_shape=(ja...  93 us
    pallas_call x1, Pallas kernels, deliver(): pl.pallas_call(functools.partial(deliver_kernel, plan, count), out_shape=...  80.5 us
    pallas_call x1, Pallas kernels, filter_lower(): pl.pallas_call(functools.partial(lower_kernel, plan), out_shape=(jax.Shap...  15.6 us
    pallas_call x1, Pallas kernels, gather(): pl.pallas_call(functools.partial(gather_kernel, plan), out_shape=jax.Shap...  10.7 us
    pallas_call x1, Pallas kernels, filter_upper(): pl.pallas_call(functools.partial(upper_kernel, plan), out_shape=(jax.Shap...  9.41 us
    pallas_call x1, Pallas kernels, transform(): pl.pallas_call(functools.partial(transform_kernel, plan), out_shape=jax.S...  8.81 us

profile of v1, /device:TPU:7, one launch (start us, length us, event | category | flops | bytes accessed | tf_op | source)
XLA Modules:
  0.0 359.9 jit_solution(2315707764106965748)
XLA Ops:
  0.0 0.0 copy-start
  0.0 2.6 shard_map.91
  2.6 1.4 fusion
  10.3 10.7 %shard_map.92 = bf16[16,8,3,2,64,128]{5,4,3,2,1,0:T(8,128)(2,1)} custom-call(s32[8]{0:T(128)} %get-tuple-element.103.meta, s32[8]{0:T(128)} %get-tuple-element.106.chosen, bf16[2,3072,1024]{2,1,0:T(8,128)(2,1)} %in_ref.1), custom_call_target="tpu_custom_call" | custom-call | tf_op jit(solution)/shard_map/pallas_call | solution.py:519
  21.0 126.1 %conditional.3 = (bf16[4,4,8,3,2,64,128]{6,5,4,3,2,1,0:T(8,128)(2,1)}) conditional(s32[]{:T(128)} %bitcast.7, bf16[16,8,3,2,64,128]{5,4,3,2,1,0:T(8,128)(2,1)} %shard_map.92, bf16[16,8,3,2,64,128]{5,4,3,2,1,0:T(8,128)(2,1)} %shard_map.92, bf16[16,8,3,2,64,128]{5,4,3,2,1,0:T(8,128)(2,1)} %shard_map.92, ...), branch_computations={%region_0.1_spmd, %region_1.2_spmd, %region_2.3_spmd, %region_3.4_... | conditional | bytes 8 | solution.py:973
  21.0 126.0 %branch_4_fun.3 = bf16[16,8,3,2,64,128]{5,4,3,2,1,0:T(8,128)(2,1)} custom-call(bf16[16,8,3,2,64,128]{5,4,3,2,1,0:T(8,128)(2,1)} %src.4), custom_call_target="tpu_custom_call" | custom-call | tf_op jit(solution)/shard_map/cond/branch_4_fun/pallas_call | solution.py:584
  147.1 0.0 copy-done
  147.1 0.1 constant_dynamic-slice_fusion
  147.2 1.3 broadcast_in_dim.6.w_ref
  151.4 9.4 %shard_map.93 = (s16[144,2,64,128]{3,2,1,0:T(8,128)(2,1)}, f32[144,128]{1,0:T(8,128)S(1)}) custom-call(s32[8]{0:T(128)} %get-tuple-element.103.meta, s32[5,16]{1,0:T(8,128)} %get-tuple-element.104.reqs, bf16[4,4,8,3,2,64,128]{6,5,4,3,2,1,0:T(8,128)(2,1)} %get-tuple-element.140.in_ref, f32[32,64,128]{2,1,0:T(8,128)} %broadcast_in_dim.6.w_ref), custom_call_target="tpu_custom_call" | custom-call | tf_op jit(solution)/shard_map/pallas_call | solution.py:672
  160.8 93.0 %conditional.4 = ((s16[144,2,64,128]{3,2,1,0:T(8,128)(2,1)}, f32[144,128]{1,0:T(8,128)S(1)})) conditional(s32[]{:T(128)} %bitcast.8, (s16[144,2,64,128]{3,2,1,0:T(8,128)(2,1)}, f32[144,128]{1,0:T(8,128)S(1)}) %shard_map.93, (s16[144,2,64,128]{3,2,1,0:T(8,128)(2,1)}, f32[144,128]{1,0:T(8,128)S(1)}) %shard_map.93, ...), branch_computations={%region_6.7_spmd, %region_7.8_spmd, %region_8.9_spmd, %region_9.10... | conditional | bytes 8 | solution.py:973
  160.8 93.0 %branch_2_fun.4 = (s16[144,2,64,128]{3,2,1,0:T(8,128)(2,1)}, f32[144,128]{1,0:T(8,128)S(1)}) custom-call(s16[144,2,64,128]{3,2,1,0:T(8,128)(2,1)} %get-tuple-element.71.src, f32[144,128]{1,0:T(8,128)S(1)} %get-tuple-element.72.src_scale), custom_call_target="tpu_custom_call" | custom-call | tf_op jit(solution)/shard_map/cond/branch_2_fun/pallas_call | solution.py:740
  253.8 15.6 %shard_map.94 = (s16[192,2,64,128]{3,2,1,0:T(8,128)(2,1)}, f32[192,128]{1,0:T(8,128)S(1)}) custom-call(s32[8]{0:T(128)} %get-tuple-element.103.meta, s32[5,16]{1,0:T(8,128)} %get-tuple-element.104.reqs, s32[144]{0:T(256)} %get-tuple-element.105.pos, bf16[4,4,8,3,2,64,128]{6,5,4,3,2,1,0:T(8,128)(2,1)} %get-tuple-element.140.in_ref, ...), custom_call_target="tpu_custom_call" | custom-call | tf_op jit(solution)/shard_map/pallas_call | solution.py:690
  269.4 0.0 copy-start.1
  269.4 80.5 %conditional.5 = ((s16[16,16,2,64,128]{4,3,2,1,0:T(8,128)(2,1)}, f32[16,16,128]{2,1,0:T(8,128)S(1)})) conditional(s32[]{:T(128)} %bitcast.6, (s16[12,16,2,64,128]{4,3,2,1,0:T(8,128)(2,1)}, f32[12,16,128]{2,1,0:T(8,128)S(1)}) %tuple.98, (s16[12,16,2,64,128]{4,3,2,1,0:T(8,128)(2,1)}, ...), branch_computations={%region_12.13_spmd, %region_13.14_spmd, %region_14.15_spmd, %regio... | conditional | bytes 8 | solution.py:973
  269.4 80.5 %branch_3_fun.5 = (s16[16,16,2,64,128]{4,3,2,1,0:T(8,128)(2,1)}, f32[16,16,128]{2,1,0:T(8,128)S(1)}) custom-call(s16[12,16,2,64,128]{4,3,2,1,0:T(8,128)(2,1)} %get-tuple-element.85.src, f32[12,16,128]{2,1,0:T(8,128)S(1)} %get-tuple-element.86.src_scale), custom_call_target="tpu_custom_call" | custom-call | tf_op jit(solution)/shard_map/cond/branch_3_fun/pallas_call | solution.py:829
  349.9 0.0 copy-done.1
  349.9 1.2 broadcast_in_dim.7.turn_ref
  351.1 8.8 %shard_map.95 = bf16[3,4,2,1024,128]{4,3,2,1,0:T(8,128)(2,1)} custom-call(s32[12]{0:T(128)} %get-tuple-element.102.omap, s16[16,16,2,64,128]{4,3,2,1,0:T(8,128)(2,1)} %get-tuple-element.111.in_ref, f32[16,16,128]{2,1,0:T(8,128)S(1)} %get-tuple-element.112.scale_ref, bf16[512,256]{1,0:T(8,128)(2,1)} %constant.78.clone.high_ref, ...), custom_call_target="tpu_custom_call" | custom-call | tf_op jit(solution)/shard_map/pallas_call | solution.py:916
  (1 shorter events, 0.0 us)
Async XLA Ops:
  0.0 147.1 %copy-start = (f32[16,1024]{1,0:T(8,128)S(1)}, f32[16,1024]{1,0:T(8,128)}, u32[]{:S(2)}) copy-start(f32[16,1024]{1,0:T(8,128)} %param.28) | copy-start | bytes 196612
  269.4 80.5 %copy-start.1 = (f32[2,3,256]{2,1,0:T(4,128)S(1)}, f32[2,3,256]{2,1,0:T(4,128)}, u32[]{:S(2)}) copy-start(f32[2,3,256]{2,1,0:T(4,128)} %constant.77.clone) | copy-start | bytes 18436
